TPU v7x, 32 devices: a whole 2x2x4 slice. The times are simulated.
32 devices in a mesh: task: 2 (over x), dp: 8 (over z, core), mp: 2 (over y).
Axes of the slice: x: 2, y: 2, z: 4, core: 2. Of those that a mesh axis runs over, the one named last changes fastest.
Arguments:
- deltas: bfloat16 [6, 2048, 4608], P('task', 'dp', 'mp'), may hold values from -400 to 400, as said below
- fishers: bfloat16 [6, 2048, 4608], P('task', 'dp', 'mp'), may hold values from 0.0009994507 to 1
Outputs:
- merged_out: float32 [2048, 4608], P('dp', 'mp')
Inputs may be any that keep to these rules, and one draw needn't show every extreme that they name: `deltas`: Real-valued weight differences.
All inputs are finite; a program needn't handle non-finite values.
Results may differ from a plain program's by a relative error of at most 0.0003.
Values sent between devices are 32-bit elements; how exact they have to be, the bound alone decides.
A program may use at most 64 MiB of HBM per device.

v0:
```python
import jax
import jax.numpy as jnp
from jax import lax
from jax.sharding import PartitionSpec as P


def task_squares(deltas):
    widened = deltas.astype(jnp.float32)
    own_sums = jnp.sum(widened * widened, axis=(1, 2))
    held_tasks = deltas.shape[0]
    slot_sums = jnp.zeros((held_tasks * lax.axis_size("task"),), jnp.float32)
    return lax.dynamic_update_slice(slot_sums, own_sums, (lax.axis_index("task") * held_tasks,))


def shards(deltas, fishers):
    weights = fishers.astype(jnp.float32)
    numerator = jnp.sum(weights * deltas.astype(jnp.float32), axis=0)
    denominator = jnp.sum(weights, axis=0)
    task_part = task_squares(deltas)
    task_sq = lax.psum(task_part, ("task", "dp", "mp"))
    numerator, denominator = (
        lax.psum_scatter(numerator, "task", scatter_dimension=0, tiled=True),
        lax.psum_scatter(denominator, "task", scatter_dimension=0, tiled=True),
    )
    half_rows = numerator / denominator
    merged_part = jnp.sum(half_rows * half_rows)
    merged = lax.all_gather(half_rows, "task", axis=0, tiled=True)
    merged_sq = lax.psum(merged_part, ("task", "dp", "mp"))
    target = jnp.mean(jnp.sqrt(task_sq + 1e-06))
    rescale = target / jnp.sqrt(merged_sq + 1e-06)
    return rescale * merged


def solution(mesh):
    placed = (P("task", "dp", "mp"), P("task", "dp", "mp"))
    return jax.shard_map(
        shards, mesh=mesh, in_specs=placed, out_specs=P("dp", "mp"), check_vma=False
    )
```

profile of v0, /device:TPU:0, one launch (start us, length us, event | category | flops | bytes accessed | tf_op | source)
XLA Modules:
  0.0 144.6 jit_solution(8158411460100088740)
XLA Ops:
  6.5 0.0 reduce-scatter.3.cloned.1.call-start
  6.5 7.8 %fusion = (f32[3]{0:T(128)S(1)}, f32[256,2304]{1,0:T(8,128)}, f32[256,2304]{1,0:T(8,128)}) fusion(bf16[3,256,2304]{2,1,0:T(8,128)(2,1)} %param.2, bf16[3,256,2304]{2,1,0:T(8,128)(2,1)} %param.3), kind=kLoop, calls=%fused_computation.3 | loop fusion | flops 11206653 | bytes 11796492 | tf_op jit(solution)/shard_map/reduce_sum | solution.py:9
  14.4 0.0 reduce-scatter.3.cloned.1.call-update
  14.4 0.0 reduce-scatter.5.cloned.1.call-start
  14.4 0.7 reduce-scatter.5.cloned.1.call-update
  15.1 0.0 all-gather.2.cloned.1.call-start
  15.2 36.9 %reduce-scatter.3.cloned.1.call-done = f32[128,2304]{1,0:T(8,128)} async-done(((f32[256,2304]{1,0:T(8,128)}), f32[128,2304]{1,0:T(8,128)}) %reduce-scatter.3.cloned.1.call-update) | async-done | bytes 1179664 | tf_op jit(solution)/shard_map/reduce_scatter | solution.py:22
  52.1 37.0 %reduce-scatter.5.cloned.1.call-done = f32[128,2304]{1,0:T(8,128)} async-done(((f32[256,2304]{1,0:T(8,128)}), f32[128,2304]{1,0:T(8,128)}) %reduce-scatter.5.cloned.1.call-update) | async-done | bytes 1179664 | tf_op jit(solution)/shard_map/reduce_scatter | solution.py:23
  89.1 3.5 %multiply_reduce_fusion = (f32[]{:T(128)}, f32[128,2304]{1,0:T(8,128)}) fusion(f32[128,2304]{1,0:T(8,128)} %reduce-scatter.3.cloned.1.call-done, f32[128,2304]{1,0:T(8,128)} %reduce-scatter.5.cloned.1.call-done), kind=kLoop, calls=%fused_computation.6 | loop fusion | flops 884735 | bytes 3538948 | tf_op jit(solution)/shard_map/reduce_sum | solution.py:26
  92.6 0.0 all-gather.2.cloned.1.call-update
  92.6 0.2 dynamic_update_slice.3
  92.9 40.1 %all-reduce = (f32[6]{0:T(128)S(1)}, f32[]{:T(128)}) all-reduce(f32[6]{0:T(128)S(1)} %dynamic_update_slice.3, f32[]{:T(128)} %get-tuple-element.10), channel_id=1, replica_groups=mesh['task'=2,'dp'=8,'mp'=2] {'task','dp','mp'}, use_global_device_ids=true, to_apply=%region_1.0 | all-reduce | flops 7 | bytes 56 | tf_op jit(solution)/shard_map/psum | solution.py:20
  133.7 0.6 sqrt_reduce_fusion
  134.8 0.0 all-gather.2.cloned.1.call-done
  134.9 3.2 %broadcast_multiply_fusion = f32[256,2304]{1,0:T(8,128)} fusion(f32[256,2304]{1,0:T(8,128)} %all-gather.2.cloned.1.call-done, f32[]{:T(128)S(6)} %div.11), kind=kLoop, calls=%fused_computation.5 | loop fusion | flops 589824 | bytes 4718596 | tf_op jit(solution)/shard_map/mul | solution.py:31
  (1 shorter events, 0.0 us)
Async XLA Ops:
  6.5 45.5 %reduce-scatter.3.cloned.1.call-start = ((), (), s32[]{:S(2)}) async-start(), calls=%async_computation.2 | async-start | bytes 3538944 | tf_op jit(solution)/shard_map/reduce_scatter | solution.py:22
  14.4 74.7 %reduce-scatter.5.cloned.1.call-start = ((), (), s32[]{:S(2)}) async-start(), calls=%async_computation.3 | async-start | bytes 3538944 | tf_op jit(solution)/shard_map/reduce_scatter | solution.py:23
  15.1 119.7 %all-gather.2.cloned.1.call-start = ((), (), s32[]{:S(2)}) async-start(), calls=%async_computation.4 | async-start | bytes 3538944 | tf_op jit(solution)/shard_map/all_gather | solution.py:27
Sparse Core Ops, SparseCore 0:
  14.5 37.5 reduce-scatter.2
  54.3 34.7 reduce-scatter.4
  92.7 36.3 all-gather.1
where the time goes:
time: 145 us
  waiting for transfers between devices  74.7 us (52%)
  blocking collectives  40.1 us (28%)
  other arithmetic  15.1 us (10%)
  between operations  14.4 us (10%)
    psum x1, blocking collectives, shards(): task_sq = lax.psum(task_part, ('task', 'dp', 'mp'))  40.1 us
    reduce_scatter x1, waiting for transfers between devices, shards(): lax.psum_scatter(denominator, 'task', scatter_dimension=0, tiled=True)  37 us
    reduce_scatter x1, waiting for transfers between devices, shards(): lax.psum_scatter(numerator, 'task', scatter_dimension=0, tiled=True)  36.9 us
    reduce_sum x1, other arithmetic, task_squares(): own_sums = jnp.sum(widened * widened, axis=(1, 2))  7.82 us
    reduce_sum x1, other arithmetic, shards(): merged_part = jnp.sum(half_rows * half_rows)  3.47 us
    mul x1, other arithmetic, shards(): return rescale * merged  3.23 us
  transfers between devices with their start and end apart: 3, of which 2 were waited for; matrix products, arithmetic and copies ran while one was open for 1% of the time, Pallas kernels for 0%

commit v1 on v0

--- a/solution.py
+++ b/solution.py
@@ -17,7 +17,7 @@
     numerator = jnp.sum(weights * deltas.astype(jnp.float32), axis=0)
     denominator = jnp.sum(weights, axis=0)
     task_part = task_squares(deltas)
-    task_sq = lax.psum(task_part, ("task", "dp", "mp"))
+    task_sq = jnp.sum(lax.all_gather(task_part, ("task", "dp", "mp")), axis=0)
     numerator, denominator = (
         lax.psum_scatter(numerator, "task", scatter_dimension=0, tiled=True),
         lax.psum_scatter(denominator, "task", scatter_dimension=0, tiled=True),

time: 145 us -> 209 us (1.44)
  blocking collectives: 40.1 us -> 104 us
    all_gather x0 -> x1, blocking collectives: none -> 67 us  [shards(): task_sq = jnp.sum(lax.all_gather(task_part, ('task', 'dp', 'mp')), axis=0)]
    psum x1, blocking collectives: 40.1 us -> 37 us  [shards(): merged_sq = lax.psum(merged_part, ('task', 'dp', 'mp'))]
  transfers between devices with their start and end apart: 3 -> 3, of which waited for: 2 -> 2; matrix products, arithmetic and copies ran while one was open for 1% -> 0% of each run, Pallas kernels for 0% -> 0%
where the time goes in v1:
time: 209 us; the launch traced here: 208 us
  blocking collectives  104 us (50%)
  waiting for transfers between devices  74.7 us (36%)
  other arithmetic  15.2 us (7%)
  between operations  14.3 us (7%)
    all_gather x1, blocking collectives, shards(): task_sq = jnp.sum(lax.all_gather(task_part, ('task', 'dp', 'mp')), axis=0)  67 us
    reduce_scatter x1, waiting for transfers between devices, shards(): lax.psum_scatter(denominator, 'task', scatter_dimension=0, tiled=True)  37 us
    psum x1, blocking collectives, shards(): merged_sq = lax.psum(merged_part, ('task', 'dp', 'mp'))  37 us
    reduce_scatter x1, waiting for transfers between devices, shards(): lax.psum_scatter(numerator, 'task', scatter_dimension=0, tiled=True)  36.9 us
    reduce_sum x1, other arithmetic, task_squares(): own_sums = jnp.sum(widened * widened, axis=(1, 2))  7.85 us
  transfers between devices with their start and end apart: 3, of which 2 were waited for; matrix products, arithmetic and copies ran while one was open for 0% of the time, Pallas kernels for 0%

profile of v1, /device:TPU:0, one launch (start us, length us, event | category | flops | bytes accessed | tf_op | source)
XLA Modules:
  0.0 208.4 jit_solution(5973919558160702079)
XLA Ops:
  6.5 0.0 reduce-scatter.3.cloned.1.call-start
  6.5 7.8 %fusion = (f32[3]{0:T(128)S(1)}, f32[256,2304]{1,0:T(8,128)}, f32[256,2304]{1,0:T(8,128)}) fusion(bf16[3,256,2304]{2,1,0:T(8,128)(2,1)} %param.2, bf16[3,256,2304]{2,1,0:T(8,128)(2,1)} %param.3), kind=kLoop, calls=%fused_computation.3 | loop fusion | flops 11206653 | bytes 11796492 | tf_op jit(solution)/shard_map/reduce_sum | solution.py:9
  14.4 0.0 reduce-scatter.3.cloned.1.call-update
  14.4 0.0 reduce-scatter.5.cloned.1.call-start
  14.5 0.7 reduce-scatter.5.cloned.1.call-update
  15.2 0.0 all-gather.3.cloned.1.call-start
  15.2 36.9 %reduce-scatter.3.cloned.1.call-done = f32[128,2304]{1,0:T(8,128)} async-done(((f32[256,2304]{1,0:T(8,128)}), f32[128,2304]{1,0:T(8,128)}) %reduce-scatter.3.cloned.1.call-update) | async-done | bytes 1179664 | tf_op jit(solution)/shard_map/reduce_scatter | solution.py:22
  52.1 37.0 %reduce-scatter.5.cloned.1.call-done = f32[128,2304]{1,0:T(8,128)} async-done(((f32[256,2304]{1,0:T(8,128)}), f32[128,2304]{1,0:T(8,128)}) %reduce-scatter.5.cloned.1.call-update) | async-done | bytes 1179664 | tf_op jit(solution)/shard_map/reduce_scatter | solution.py:23
  89.1 3.4 %multiply_reduce_fusion = (f32[]{:T(128)}, f32[128,2304]{1,0:T(8,128)}) fusion(f32[128,2304]{1,0:T(8,128)} %reduce-scatter.3.cloned.1.call-done, f32[128,2304]{1,0:T(8,128)} %reduce-scatter.5.cloned.1.call-done), kind=kLoop, calls=%fused_computation.6 | loop fusion | flops 884735 | bytes 3538948 | tf_op jit(solution)/shard_map/reduce_sum | solution.py:26
  92.6 0.0 all-gather.3.cloned.1.call-update
  92.6 0.1 dynamic_update_slice.5
  92.8 67.0 %all-gather = f32[32,1,6]{2,1,0:T(1,128)S(1)} all-gather(f32[1,1,6]{2,1,0:T(1,128)S(1)} %dynamic_update_slice.5), channel_id=1, replica_groups=mesh['task'=2,'dp'=8,'mp'=2] {'task','dp','mp'}, dimensions={0}, use_global_device_ids=true | all-gather | bytes 792 | tf_op jit(solution)/shard_map/all_gather | solution.py:20
  159.8 0.1 reduce_sum.55
  159.8 0.6 sqrt_reduce_fusion
  161.0 37.0 %psum.7 = f32[]{:T(128)} all-reduce(f32[]{:T(128)} %get-tuple-element.8), channel_id=1, replica_groups=mesh['task'=2,'dp'=8,'mp'=2] {'task','dp','mp'}, use_global_device_ids=true, to_apply=%region_8.0 | all-reduce | flops 1 | bytes 8 | tf_op jit(solution)/shard_map/psum | solution.py:28
  198.6 0.0 all-gather.3.cloned.1.call-done
  198.7 3.2 %broadcast_multiply_fusion = f32[256,2304]{1,0:T(8,128)} fusion(f32[256,2304]{1,0:T(8,128)} %all-gather.3.cloned.1.call-done, f32[]{:T(128)S(6)} %div.11), kind=kLoop, calls=%fused_computation.5 | loop fusion | flops 589824 | bytes 4718596 | tf_op jit(solution)/shard_map/mul | solution.py:31
  (1 shorter events, 0.0 us)
Async XLA Ops:
  6.5 45.6 %reduce-scatter.3.cloned.1.call-start = ((), (), s32[]{:S(2)}) async-start(), calls=%async_computation.2 | async-start | bytes 3538944 | tf_op jit(solution)/shard_map/reduce_scatter | solution.py:22
  14.4 74.7 %reduce-scatter.5.cloned.1.call-start = ((), (), s32[]{:S(2)}) async-start(), calls=%async_computation.3 | async-start | bytes 3538944 | tf_op jit(solution)/shard_map/reduce_scatter | solution.py:23
  15.2 183.5 %all-gather.3.cloned.1.call-start = ((), (), s32[]{:S(2)}) async-start(), calls=%async_computation.4 | async-start | bytes 3538944 | tf_op jit(solution)/shard_map/all_gather | solution.py:27
Sparse Core Ops, SparseCore 0:
  14.5 37.5 reduce-scatter.2
  54.3 34.7 reduce-scatter.4
  92.7 36.0 all-gather.2

commit v2 on v0

--- a/solution.py
+++ b/solution.py
@@ -17,7 +17,7 @@
     numerator = jnp.sum(weights * deltas.astype(jnp.float32), axis=0)
     denominator = jnp.sum(weights, axis=0)
     task_part = task_squares(deltas)
-    task_sq = lax.psum(task_part, ("task", "dp", "mp"))
+    task_sq = lax.psum(lax.psum(task_part, ("dp", "mp")), "task")
     numerator, denominator = (
         lax.psum_scatter(numerator, "task", scatter_dimension=0, tiled=True),
         lax.psum_scatter(denominator, "task", scatter_dimension=0, tiled=True),

time: 145 us -> 180 us (1.24)
  blocking collectives: 40.1 us -> 74.9 us
    psum x1 -> x3, blocking collectives: 40.1 us -> 74.9 us  [the longest x2 37.9 us: shards(): task_sq = lax.psum(lax.psum(task_part, ('dp', 'mp')), 'task')]
  transfers between devices with their start and end apart: 3 -> 3, of which waited for: 2 -> 2; matrix products, arithmetic and copies ran while one was open for 1% -> 0% of each run, Pallas kernels for 0% -> 0%
where the time goes in v2:
time: 180 us; the launch traced here: 179 us
  blocking collectives  74.9 us (42%)
  waiting for transfers between devices  74.7 us (42%)
  other arithmetic  15.1 us (8%)
  between operations  14.3 us (8%)
    psum x2, blocking collectives, shards(): task_sq = lax.psum(lax.psum(task_part, ('dp', 'mp')), 'task')  37.9 us
    reduce_scatter x1, waiting for transfers between devices, shards(): lax.psum_scatter(denominator, 'task', scatter_dimension=0, tiled=True)  37 us
    psum x1, blocking collectives, shards(): merged_sq = lax.psum(merged_part, ('task', 'dp', 'mp'))  37 us
    reduce_scatter x1, waiting for transfers between devices, shards(): lax.psum_scatter(numerator, 'task', scatter_dimension=0, tiled=True)  36.9 us
    reduce_sum x1, other arithmetic, task_squares(): own_sums = jnp.sum(widened * widened, axis=(1, 2))  7.85 us
  transfers between devices with their start and end apart: 3, of which 2 were waited for; matrix products, arithmetic and copies ran while one was open for 0% of the time, Pallas kernels for 0%

profile of v2, /device:TPU:0, one launch (start us, length us, event | category | flops | bytes accessed | tf_op | source)
XLA Modules:
  0.0 179.3 jit_solution(15639292712771598451)
XLA Ops:
  6.5 0.0 reduce-scatter.3.cloned.1.call-start
  6.5 7.8 %fusion = (f32[3]{0:T(128)S(1)}, f32[256,2304]{1,0:T(8,128)}, f32[256,2304]{1,0:T(8,128)}) fusion(bf16[3,256,2304]{2,1,0:T(8,128)(2,1)} %param.2, bf16[3,256,2304]{2,1,0:T(8,128)(2,1)} %param.3), kind=kLoop, calls=%fused_computation.3 | loop fusion | flops 11206653 | bytes 11796492 | tf_op jit(solution)/shard_map/reduce_sum | solution.py:9
  14.4 0.0 reduce-scatter.3.cloned.1.call-update
  14.4 0.0 reduce-scatter.5.cloned.1.call-start
  14.5 0.7 reduce-scatter.5.cloned.1.call-update
  15.2 0.0 all-gather.2.cloned.1.call-start
  15.2 36.9 %reduce-scatter.3.cloned.1.call-done = f32[128,2304]{1,0:T(8,128)} async-done(((f32[256,2304]{1,0:T(8,128)}), f32[128,2304]{1,0:T(8,128)}) %reduce-scatter.3.cloned.1.call-update) | async-done | bytes 1179664 | tf_op jit(solution)/shard_map/reduce_scatter | solution.py:22
  52.1 37.0 %reduce-scatter.5.cloned.1.call-done = f32[128,2304]{1,0:T(8,128)} async-done(((f32[256,2304]{1,0:T(8,128)}), f32[128,2304]{1,0:T(8,128)}) %reduce-scatter.5.cloned.1.call-update) | async-done | bytes 1179664 | tf_op jit(solution)/shard_map/reduce_scatter | solution.py:23
  89.1 3.4 %multiply_reduce_fusion = (f32[]{:T(128)}, f32[128,2304]{1,0:T(8,128)}) fusion(f32[128,2304]{1,0:T(8,128)} %reduce-scatter.3.cloned.1.call-done, f32[128,2304]{1,0:T(8,128)} %reduce-scatter.5.cloned.1.call-done), kind=kLoop, calls=%fused_computation.6 | loop fusion | flops 884735 | bytes 3538948 | tf_op jit(solution)/shard_map/reduce_sum | solution.py:26
  92.6 0.0 all-gather.2.cloned.1.call-update
  92.6 0.2 dynamic_update_slice.3
  92.9 33.0 %psum.21 = f32[6]{0:T(128)S(1)} all-reduce(f32[6]{0:T(128)S(1)} %dynamic_update_slice.3), channel_id=1, replica_groups=mesh['task'=2,'dp'=8,'mp'=2] {'dp','mp'}, use_global_device_ids=true, to_apply=%region_1.0 | all-reduce | flops 6 | bytes 48 | tf_op jit(solution)/shard_map/psum | solution.py:20
  125.8 4.9 %psum.22 = f32[6]{0:T(128)S(1)} all-reduce(f32[6]{0:T(128)S(1)} %psum.21), channel_id=1, replica_groups=mesh['task'=2,'dp'=8,'mp'=2] {'task'}, use_global_device_ids=true, to_apply=%region_2.0 | all-reduce | flops 6 | bytes 48 | tf_op jit(solution)/shard_map/psum | solution.py:20
  130.8 0.6 sqrt_reduce_fusion
  131.9 37.0 %psum.23 = f32[]{:T(128)} all-reduce(f32[]{:T(128)} %get-tuple-element.8), channel_id=1, replica_groups=mesh['task'=2,'dp'=8,'mp'=2] {'task','dp','mp'}, use_global_device_ids=true, to_apply=%region_9.0 | all-reduce | flops 1 | bytes 8 | tf_op jit(solution)/shard_map/psum | solution.py:28
  169.5 0.0 all-gather.2.cloned.1.call-done
  169.6 3.2 %broadcast_multiply_fusion = f32[256,2304]{1,0:T(8,128)} fusion(f32[256,2304]{1,0:T(8,128)} %all-gather.2.cloned.1.call-done, f32[]{:T(128)S(6)} %div.11), kind=kLoop, calls=%fused_computation.5 | loop fusion | flops 589824 | bytes 4718596 | tf_op jit(solution)/shard_map/mul | solution.py:31
  (1 shorter events, 0.0 us)
Async XLA Ops:
  6.5 45.6 %reduce-scatter.3.cloned.1.call-start = ((), (), s32[]{:S(2)}) async-start(), calls=%async_computation.2 | async-start | bytes 3538944 | tf_op jit(solution)/shard_map/reduce_scatter | solution.py:22
  14.4 74.7 %reduce-scatter.5.cloned.1.call-start = ((), (), s32[]{:S(2)}) async-start(), calls=%async_computation.3 | async-start | bytes 3538944 | tf_op jit(solution)/shard_map/reduce_scatter | solution.py:23
  15.2 154.4 %all-gather.2.cloned.1.call-start = ((), (), s32[]{:S(2)}) async-start(), calls=%async_computation.4 | async-start | bytes 3538944 | tf_op jit(solution)/shard_map/all_gather | solution.py:27
Sparse Core Ops, SparseCore 0:
  14.5 37.5 reduce-scatter.2
  54.3 34.7 reduce-scatter.4
  92.7 36.0 all-gather.1
